TPU v7x, 32 devices: a whole 2x2x4 slice. The times are simulated.
32 devices in a mesh: groups: 2 (over y), dom: 4 (over z), sub: 2 (over x), field: 2 (over core).
Axes of the slice: x: 2, y: 2, z: 4, core: 2. Of those that a mesh axis runs over, the one named last changes fastest.
Arguments:
- background: float32 [3, 65536], P(None, ('groups', 'dom', 'sub')), parts along dimension 1, may hold values from -6 to 6
- obs_weight: float32 [65536], P(('groups', 'dom', 'sub')), parts along dimension 0, may hold values from 0.02 to 0.2
- connect: int32 [10, 32768], P(None, ('groups', 'dom', 'sub', 'field')), parts along dimension 1, may hold values from 0 to 5631, as said below
- live_blocks: int32 [32], P(('groups', 'dom', 'sub', 'field')), parts along dimension 0, may hold values from 2 to 8, as said below
- elem_scale: float32 [32768], P(('groups', 'dom', 'sub', 'field')), parts along dimension 0, may hold values from 0.5 to 2
- reg_weight: float32 [32768], P(('groups', 'dom', 'sub', 'field')), parts along dimension 0, may hold values from 0.2 to 2
- iterate: float32 [32768], P(('groups', 'dom', 'sub', 'field')), parts along dimension 0, may hold values from -6 to 6
- residual: float32 [32768], P(('groups', 'dom', 'sub', 'field')), parts along dimension 0, may hold values from -30 to 30
- direction: float32 [32768], P(('groups', 'dom', 'sub', 'field')), parts along dimension 0, may hold values from -30 to 30
- send_nodes: int32 [16, 3, 2, 256], P(('groups', 'dom', 'sub')), parts along dimension 0, may hold values from 0 to 4095, as said below
- send_count: int32 [16, 3, 2], P(('groups', 'dom', 'sub')), parts along dimension 0, may hold values from 0 to 256, as said below
- ref_stiff: float32 [30, 30], replicated, may hold values from -1.05 to 4.05, as said below
Outputs:
- iterate_next: float32 [32768], P(('groups', 'dom', 'sub', 'field')), parts along dimension 0
- residual_next: float32 [32768], P(('groups', 'dom', 'sub', 'field')), parts along dimension 0
- direction_next: float32 [32768], P(('groups', 'dom', 'sub', 'field')), parts along dimension 0
There are 2 independent parts, one for each index of `groups`. A program takes and returns all parts, laid end to end along the dimension named above; an argument that names none is the same for every part. Nothing has to cross between parts.
Inputs may be any that keep to these rules, and one draw needn't show every extreme that they name: `send_nodes`: for every link the first send_count slots hold distinct owned nodes; later slots are padding. `send_count`: links go only to partitions of dom index d - 1, d or d + 1 and never to the sender itself or past the ends of dom; some link is full with 256 slots. `connect`: entries from 4096 on name ghost slots that are live slots of their owner's link. `live_blocks`: live blocks fill a device's slots from its first one; some device has 8. `ref_stiff`: Symmetric.
All inputs are finite; a program needn't handle non-finite values.
Results may differ from a plain program's by a relative error of at most 0.00005.
Values sent between devices are 32-bit elements; how exact they have to be, the bound alone decides.
A program may use at most 64 MiB of HBM per device.

v0:
```python
import jax
import jax.numpy as jnp
from jax import lax
from jax.sharding import PartitionSpec as P

BLK = 128


def extended(cells, sides, width):
    for axis, dim in sides:
        count = lax.axis_size(axis)
        ends = count - 1
        head = lax.slice_in_dim(cells, 0, width, axis=dim)
        tail = lax.slice_in_dim(cells, cells.shape[dim] - width, cells.shape[dim], axis=dim)
        cells = jnp.concatenate(
            [
                lax.ppermute(tail, axis, [(i, (i + 1) % count) for i in range(ends)]),
                cells,
                lax.ppermute(head, axis, [((i + 1) % count, i) for i in range(ends)]),
            ],
            axis=dim,
        )
    return cells


def on_device(
    background,
    obs_weight,
    connect,
    live_blocks,
    elem_scale,
    reg_weight,
    iterate,
    residual,
    direction,
    send_nodes,
    send_count,
    ref_stiff,
):
    owned_nodes = background.shape[1]
    sub_count = lax.axis_size("sub")
    link_slots = send_nodes.shape[3]
    element_count = connect.shape[1]
    ghost_slots = 3 * sub_count * link_slots
    targets = send_nodes[0].reshape(-1)
    open_slot = (
        jnp.arange(link_slots, dtype=jnp.int32)[None, None, :] < send_count[0][:, :, None]
    ).astype(jnp.float32)

    def fetch_ghosts(values):
        outbound = values[:, targets].reshape(3, 3, sub_count, link_slots) * open_slot[None]
        mixed = lax.all_to_all(outbound, "sub", split_axis=2, concat_axis=2, tiled=True)
        rimmed = extended(mixed, (("dom", 1),), 1)
        arrived = rimmed[:, 0::2]
        return jnp.concatenate([values, arrived.reshape(3, ghost_slots)], axis=1)

    element = jnp.arange(element_count, dtype=jnp.int32)
    live_mask = (element < BLK * live_blocks[0]).astype(jnp.float32)
    search = live_mask * direction
    remain = live_mask * residual
    guess = live_mask * iterate
    flat_connect = connect.reshape(-1)
    state_full = fetch_ghosts(background)
    element_state = state_full[:, connect].reshape(30, element_count)
    coupled = (live_mask * elem_scale)[None, :] * jnp.dot(
        ref_stiff, element_state, precision=lax.Precision.HIGHEST
    )
    terms = (search[None, :] * coupled).reshape(3, -1)
    accumulated = (
        jnp.zeros((3, owned_nodes + ghost_slots), jnp.float32).at[:, flat_connect].add(terms)
    )
    accumulated = lax.psum(accumulated, "field")
    returning = accumulated[:, owned_nodes:].reshape(3, 3, sub_count, link_slots)
    rimmed = extended(returning, (("dom", 1),), 1)
    landed = lax.all_to_all(rimmed[:, 0::2], "sub", split_axis=2, concat_axis=2, tiled=True)
    landed = (landed * open_slot[None]).reshape(3, -1)
    assembled = accumulated[:, :owned_nodes] + jnp.zeros((3, owned_nodes), jnp.float32).at[
        :, targets
    ].add(landed)
    weighted = obs_weight[None, :] * assembled
    weighted_full = fetch_ghosts(weighted)
    pulled = weighted_full[:, connect].reshape(30, element_count)
    hess_search = jnp.sum(coupled * pulled, axis=0) + reg_weight * search
    squared_before, curvature_sum, cross_term, image_square = lax.psum(
        (
            jnp.sum(remain * remain),
            jnp.sum(search * hess_search),
            jnp.sum(remain * hess_search),
            jnp.sum(hess_search * hess_search),
        ),
        ("dom", "sub", "field"),
    )
    step_length = squared_before / curvature_sum
    iterate_next = guess + step_length * search
    residual_next = remain - step_length * hess_search
    squared_after = (
        squared_before - 2.0 * step_length * cross_term + step_length * step_length * image_square
    )
    direction_next = residual_next + squared_after / squared_before * search
    return (iterate_next, residual_next, direction_next)


def solution(mesh):
    placed = (
        P(None, ("groups", "dom", "sub")),
        P(("groups", "dom", "sub")),
        P(None, ("groups", "dom", "sub", "field")),
        P(("groups", "dom", "sub", "field")),
        P(("groups", "dom", "sub", "field")),
        P(("groups", "dom", "sub", "field")),
        P(("groups", "dom", "sub", "field")),
        P(("groups", "dom", "sub", "field")),
        P(("groups", "dom", "sub", "field")),
        P(("groups", "dom", "sub"), None, None, None),
        P(("groups", "dom", "sub"), None, None),
        P(),
    )
    return jax.shard_map(
        on_device,
        mesh=mesh,
        in_specs=placed,
        out_specs=(
            P(("groups", "dom", "sub", "field")),
            P(("groups", "dom", "sub", "field")),
            P(("groups", "dom", "sub", "field")),
        ),
        check_vma=False,
    )
```

profile of v0, /device:TPU:0, one launch (start us, length us, event | category | flops | bytes accessed | tf_op | source)
XLA Modules:
  0.0 283.6 jit_solution(14023031561616133790)
XLA Ops:
  7.2 0.8 reshape_squeeze.3
  8.0 0.8 fusion.4
  8.8 1.5 copy.66
  10.3 2.6 gather_fusion
  13.8 4.2 %all-to-all-start = ((f32[3,3,2,256]{3,1,0,2:T(4,128)}), f32[3,3,2,256]{3,1,0,2:T(4,128)S(1)}, u32[]{:S(2)}, u32[]{:S(2)}) async-start(f32[3,3,2,256]{3,1,0,2:T(4,128)} %broadcast_multiply_fusion.4), calls=%async_computation | async-start | bytes 49152 | tf_op jit(solution)/shard_map/all_to_all | solution.py:52
  18.9 3.1 %all-to-all-done = f32[3,3,2,256]{3,1,0,2:T(4,128)S(1)} async-done(((f32[3,3,2,256]{3,1,0,2:T(4,128)}), f32[3,3,2,256]{3,1,0,2:T(4,128)S(1)}, u32[]{:S(2)}, u32[]{:S(2)}) %all-to-all-start) | async-done | bytes 18464 | tf_op jit(solution)/shard_map/all_to_all | solution.py:52
  22.0 4.0 %collective-permute-start = (f32[3,1,2,256]{3,1,0,2:T(1,128)S(1)}, f32[3,1,2,256]{3,1,0,2:T(1,128)S(1)}, u32[]{:S(2)}, u32[]{:S(2)}) collective-permute-start(f32[3,1,2,256]{3,1,0,2:T(1,128)S(1)} %get-tuple-element.18), channel_id=1, source_target_pairs={{0,4},{4,8},{8,12},{1,5},{5,9},{9,13},{2,6},{6,10},{10,14},{3,7},{... | collective-permute-start | bytes 18440 | tf_op jit(solution)/shard_map/ppermute | solution.py:17
  25.9 1.3 collective-permute-start.1
  27.3 4.1 %collective-permute-done.1 = f32[3,1,2,256]{3,1,0,2:T(1,128)S(1)} collective-permute-done((f32[3,1,2,256]{3,1,0,2:T(1,128)S(1)}, f32[3,1,2,256]{3,1,0,2:T(1,128)S(1)}, u32[]{:S(2)}, u32[]{:S(2)}) %collective-permute-start.1) | collective-permute-done | bytes 6176 | tf_op jit(solution)/shard_map/ppermute | solution.py:19
  31.6 0.8 copy.71
  32.4 34.2 %gather_fusion.1 = f32[10240,3]{1,0:T(8,128)} fusion(f32[3,5632]{0,1:T(8,128)S(1)} %copy.71, s32[10240]{0:T(1024)S(1)} %broadcast_clamp_fusion), kind=kCustom, calls=%fused_computation.1 | custom fusion | bytes 286720 | tf_op jit(solution)/shard_map/gather | solution.py:64
  66.7 4.2 %copy.72 = f32[10,1024,3]{1,0,2:T(8,128)S(1)} copy(f32[10,1024,3]{2,1,0:T(8,128)} %bitcast.28) | data formatting | bytes 245760 | tf_op jit(solution)/shard_map/gather | solution.py:64
  71.3 3.1 %copy.73 = f32[3,10240]{0,1:T(8,128)} copy(f32[3,10240]{1,0:T(4,128)S(1)} %reshape.145) | data formatting | bytes 245760 | tf_op jit(solution)/shard_map/reshape | solution.py:68
  74.4 51.9 %scatter_custom_fusion = f32[3,5632]{0,1:T(8,128)} fusion(s32[10240]{0:T(1024)S(1)} %bitcast.38, f32[3,10240]{0,1:T(8,128)} %copy.73, f32[]{:T(128)} %constant.7.clone.1), kind=kCustom, calls=%fused_computation.6 | custom fusion | flops 30720 | bytes 190468 | tf_op jit(solution)/shard_map/scatter-add | solution.py:70
  126.3 22.3 %all-reduce.3.cloned.1.call-done = f32[3,5632]{0,1:T(8,128)} async-done(((f32[3,5632]{0,1:T(8,128)}), f32[3,5632]{0,1:T(8,128)}) %all-reduce.3.cloned.1.call-update) | async-done | bytes 67600 | tf_op jit(solution)/shard_map/psum | solution.py:72
  148.6 1.2 slice.55
  150.1 3.8 %collective-permute-start.2 = (f32[3,1,2,256]{3,1,0,2:T(1,128)S(1)}, f32[3,1,2,256]{3,1,0,2:T(1,128)S(1)}, u32[]{:S(2)}, u32[]{:S(2)}) collective-permute-start(f32[3,1,2,256]{3,1,0,2:T(1,128)S(1)} %get-tuple-element.16), channel_id=1, source_target_pairs={{0,4},{4,8},{8,12},{1,5},{5,9},{9,13},{2,6},{6,10},{10,14},{3,7},{... | collective-permute-start | bytes 18440 | tf_op jit(solution)/shard_map/ppermute | solution.py:17
  153.9 1.3 collective-permute-start.3
  155.2 4.2 %collective-permute-done.3 = f32[3,1,2,256]{3,1,0,2:T(1,128)S(1)} collective-permute-done((f32[3,1,2,256]{3,1,0,2:T(1,128)S(1)}, f32[3,1,2,256]{3,1,0,2:T(1,128)S(1)}, u32[]{:S(2)}, u32[]{:S(2)}) %collective-permute-start.3) | collective-permute-done | bytes 6176 | tf_op jit(solution)/shard_map/ppermute | solution.py:19
  160.1 3.2 %all-to-all-start.1 = ((f32[3,3,2,256]{3,1,0,2:T(4,128)}), f32[3,3,2,256]{3,1,0,2:T(4,128)S(1)}, u32[]{:S(2)}, u32[]{:S(2)}) async-start(f32[3,3,2,256]{3,1,0,2:T(4,128)} %slice.40), calls=%async_computation.1 | async-start | bytes 49152 | tf_op jit(solution)/shard_map/all_to_all | solution.py:75
  163.4 3.9 %all-to-all-done.1 = f32[3,3,2,256]{3,1,0,2:T(4,128)S(1)} async-done(((f32[3,3,2,256]{3,1,0,2:T(4,128)}), f32[3,3,2,256]{3,1,0,2:T(4,128)S(1)}, u32[]{:S(2)}, u32[]{:S(2)}) %all-to-all-start.1) | async-done | bytes 18464 | tf_op jit(solution)/shard_map/all_to_all | solution.py:75
  167.6 9.5 %scatter_fusion = f32[3,4096]{0,1:T(8,128)S(1)} fusion(f32[3,4096]{0,1:T(8,128)S(1)} %slice-done, s32[1536]{0:T(1024)S(1)} %fusion.5, f32[1536,3]{1,0:T(8,128)S(1)} %copy.78), kind=kCustom, calls=%fused_computation.5 | custom fusion | flops 4608 | bytes 61440 | tf_op jit(solution)/shard_map/scatter-add | solution.py:79
  177.2 1.9 broadcast_multiply_fusion
  179.1 4.3 %gather_fusion.2 = f32[1536,3]{1,0:T(8,128)S(1)} fusion(f32[3,4096]{0,1:T(8,128)} %broadcast_multiply_fusion, s32[2048]{0:T(1024)S(1)} %pad_clamp_fusion), kind=kCustom, calls=%fused_computation.2 | custom fusion | bytes 43008 | tf_op jit(solution)/shard_map/gather | solution.py:51
  183.8 6.3 %all_to_all.15 = f32[3,3,2,256]{3,1,0,2:T(4,128)S(1)} all-to-all(f32[3,3,2,256]{3,1,0,2:T(4,128)S(1)} %broadcast_multiply_fusion.2), channel_id=1, replica_groups=mesh['groups'=2,'dom'=4,'sub'=2,'field'=2] {'sub'}, dimensions={2} | all-to-all | bytes 36864 | tf_op jit(solution)/shard_map/all_to_all | solution.py:52
  190.1 3.4 %collective-permute-start.4 = (f32[3,1,2,256]{3,1,0,2:T(1,128)S(1)}, f32[3,1,2,256]{3,1,0,2:T(1,128)S(1)}, u32[]{:S(2)}, u32[]{:S(2)}) collective-permute-start(f32[3,1,2,256]{3,1,0,2:T(1,128)S(1)} %get-tuple-element.14), channel_id=1, source_target_pairs={{0,4},{4,8},{8,12},{1,5},{5,9},{9,13},{2,6},{6,10},{10,14},{3,7},{... | collective-permute-start | bytes 18440 | tf_op jit(solution)/shard_map/ppermute | solution.py:17
  193.5 1.3 collective-permute-start.5
  194.8 4.2 %collective-permute-done.5 = f32[3,1,2,256]{3,1,0,2:T(1,128)S(1)} collective-permute-done((f32[3,1,2,256]{3,1,0,2:T(1,128)S(1)}, f32[3,1,2,256]{3,1,0,2:T(1,128)S(1)}, u32[]{:S(2)}, u32[]{:S(2)}) %collective-permute-start.5) | collective-permute-done | bytes 6176 | tf_op jit(solution)/shard_map/ppermute | solution.py:19
  199.3 1.7 pad_maximum_fusion
  201.1 36.1 %gather_fusion.3 = f32[10240,3]{1,0:T(8,128)} fusion(f32[3,5632]{0,1:T(8,128)} %pad_maximum_fusion, s32[10240]{0:T(1024)S(1)} %broadcast_clamp_fusion), kind=kCustom, calls=%fused_computation.3 | custom fusion | bytes 286720 | tf_op jit(solution)/shard_map/gather | solution.py:82
  237.1 4.2 %copy.84 = f32[10,1024,3]{1,0,2:T(8,128)S(1)} copy(f32[10,1024,3]{2,1,0:T(8,128)} %bitcast.27) | data formatting | bytes 245760 | tf_op jit(solution)/shard_map/gather | solution.py:82
  242.1 30.1 %all-reduce = (f32[]{:T(128)}, f32[]{:T(128)}, f32[]{:T(128)}, f32[]{:T(128)}) all-reduce(f32[]{:T(128)} %get-tuple-element.5, f32[]{:T(128)} %get-tuple-element.6, f32[]{:T(128)} %get-tuple-element.4, f32[]{:T(128)} %get-tuple-element.3), channel_id=1, replica_groups=mesh['groups'=2,'dom'=4,'sub'=2,'field'=2] {'dom','sub','field'}, use_global_device_ids=true, to_apply=%region_1.0 | all-reduce | flops 4 | bytes 32 | tf_op jit(solution)/shard_map/psum | solution.py:84
  (69 shorter events, 5.0 us)
Async XLA Ops:
  7.2 63.7 %copy-start = (f32[30,30]{1,0:T(8,128)S(1)}, f32[30,30]{1,0:T(8,128)}, u32[]{:S(2)}) copy-start(f32[30,30]{1,0:T(8,128)} %param.23) | copy-start | bytes 10804
  7.2 24.4 %copy-start.2 = (f32[3,4096]{1,0:T(4,128)S(1)}, f32[3,4096]{1,0:T(4,128)}, u32[]{:S(2)}) copy-start(f32[3,4096]{1,0:T(4,128)} %param.12) | copy-start | bytes 147460
  7.2 10.9 %copy-start.3 = (s32[10,1024]{1,0:T(8,128)S(1)}, s32[10,1024]{1,0:T(8,128)}, u32[]{:S(2)}) copy-start(s32[10,1024]{1,0:T(8,128)} %param.14) | copy-start | bytes 122884
  7.2 20.0 %copy-start.7 = (f32[1024]{0:T(1024)S(1)}, f32[1024]{0:T(1024)}, u32[]{:S(2)}) copy-start(f32[1024]{0:T(1024)} %param.20) | copy-start | bytes 12292
  7.2 20.0 %copy-start.6 = (f32[1024]{0:T(1024)S(1)}, f32[1024]{0:T(1024)}, u32[]{:S(2)}) copy-start(f32[1024]{0:T(1024)} %param.16) | copy-start | bytes 12292
  13.8 8.1 %all-to-all-start = ((f32[3,3,2,256]{3,1,0,2:T(4,128)}), f32[3,3,2,256]{3,1,0,2:T(4,128)S(1)}, u32[]{:S(2)}, u32[]{:S(2)}) async-start(f32[3,3,2,256]{3,1,0,2:T(4,128)} %broadcast_multiply_fusion.4), calls=%async_computation | async-start | bytes 49152 | tf_op jit(solution)/shard_map/all_to_all | solution.py:52
  18.1 130.5 %all-reduce.3.cloned.1.call-start = ((), (), s32[]{:S(2)}) async-start(), calls=%async_computation.3 | async-start | bytes 5767168 | tf_op jit(solution)/shard_map/psum | solution.py:72
  22.0 5.3 %collective-permute-start = (f32[3,1,2,256]{3,1,0,2:T(1,128)S(1)}, f32[3,1,2,256]{3,1,0,2:T(1,128)S(1)}, u32[]{:S(2)}, u32[]{:S(2)}) collective-permute-start(f32[3,1,2,256]{3,1,0,2:T(1,128)S(1)} %get-tuple-element.18), channel_id=1, source_target_pairs={{0,4},{4,8},{8,12},{1,5},{5,9},{9,13},{2,6},{6,10},{10,14},{3,7},{... | collective-permute-start | bytes 18440 | tf_op jit(solution)/shard_map/ppermute | solution.py:17
  25.9 5.5 %collective-permute-start.1 = (f32[3,1,2,256]{3,1,0,2:T(1,128)S(1)}, f32[3,1,2,256]{3,1,0,2:T(1,128)S(1)}, u32[]{:S(2)}, u32[]{:S(2)}) collective-permute-start(f32[3,1,2,256]{3,1,0,2:T(1,128)S(1)} %get-tuple-element.19), channel_id=1, source_target_pairs={{4,0},{8,4},{12,8},{5,1},{9,5},{13,9},{6,2},{10,6},{14,10},{7,3},{... | collective-permute-start | bytes 18440 | tf_op jit(solution)/shard_map/ppermute | solution.py:19
  150.1 17.5 %slice-start = ((f32[3,5632]{0,1:T(8,128)}), f32[3,4096]{0,1:T(8,128)S(1)}, s32[]{:S(2)}) async-start(f32[3,5632]{0,1:T(8,128)} %all-reduce.3.cloned.1.call-done), calls=%async_computation.4 | async-start | bytes 4194304 | tf_op jit(solution)/shard_map/slice | solution.py:77
  150.1 27.0 %copy-start.4 = (f32[4096]{0:T(1024)S(1)}, f32[4096]{0:T(1024)}, u32[]{:S(2)}) copy-start(f32[4096]{0:T(1024)} %param.13) | copy-start | bytes 49156
  150.1 5.1 %collective-permute-start.2 = (f32[3,1,2,256]{3,1,0,2:T(1,128)S(1)}, f32[3,1,2,256]{3,1,0,2:T(1,128)S(1)}, u32[]{:S(2)}, u32[]{:S(2)}) collective-permute-start(f32[3,1,2,256]{3,1,0,2:T(1,128)S(1)} %get-tuple-element.16), channel_id=1, source_target_pairs={{0,4},{4,8},{8,12},{1,5},{5,9},{9,13},{2,6},{6,10},{10,14},{3,7},{... | collective-permute-start | bytes 18440 | tf_op jit(solution)/shard_map/ppermute | solution.py:17
  153.9 5.5 %collective-permute-start.3 = (f32[3,1,2,256]{3,1,0,2:T(1,128)S(1)}, f32[3,1,2,256]{3,1,0,2:T(1,128)S(1)}, u32[]{:S(2)}, u32[]{:S(2)}) collective-permute-start(f32[3,1,2,256]{3,1,0,2:T(1,128)S(1)} %get-tuple-element.17), channel_id=1, source_target_pairs={{4,0},{8,4},{12,8},{5,1},{9,5},{13,9},{6,2},{10,6},{14,10},{7,3},{... | collective-permute-start | bytes 18440 | tf_op jit(solution)/shard_map/ppermute | solution.py:19
  160.1 7.1 %all-to-all-start.1 = ((f32[3,3,2,256]{3,1,0,2:T(4,128)}), f32[3,3,2,256]{3,1,0,2:T(4,128)S(1)}, u32[]{:S(2)}, u32[]{:S(2)}) async-start(f32[3,3,2,256]{3,1,0,2:T(4,128)} %slice.40), calls=%async_computation.1 | async-start | bytes 49152 | tf_op jit(solution)/shard_map/all_to_all | solution.py:75
  179.1 20.2 %copy-start.1 = (f32[3,4096]{0,1:T(8,128)S(1)}, f32[3,4096]{0,1:T(8,128)}, u32[]{:S(2)}) copy-start(f32[3,4096]{0,1:T(8,128)} %broadcast_multiply_fusion) | copy-start | bytes 147460
  190.1 4.7 %collective-permute-start.4 = (f32[3,1,2,256]{3,1,0,2:T(1,128)S(1)}, f32[3,1,2,256]{3,1,0,2:T(1,128)S(1)}, u32[]{:S(2)}, u32[]{:S(2)}) collective-permute-start(f32[3,1,2,256]{3,1,0,2:T(1,128)S(1)} %get-tuple-element.14), channel_id=1, source_target_pairs={{0,4},{4,8},{8,12},{1,5},{5,9},{9,13},{2,6},{6,10},{10,14},{3,7},{... | collective-permute-start | bytes 18440 | tf_op jit(solution)/shard_map/ppermute | solution.py:17
  193.5 5.5 %collective-permute-start.5 = (f32[3,1,2,256]{3,1,0,2:T(1,128)S(1)}, f32[3,1,2,256]{3,1,0,2:T(1,128)S(1)}, u32[]{:S(2)}, u32[]{:S(2)}) collective-permute-start(f32[3,1,2,256]{3,1,0,2:T(1,128)S(1)} %get-tuple-element.15), channel_id=1, source_target_pairs={{4,0},{8,4},{12,8},{5,1},{9,5},{13,9},{6,2},{10,6},{14,10},{7,3},{... | collective-permute-start | bytes 18440 | tf_op jit(solution)/shard_map/ppermute | solution.py:19
  237.1 4.3 %copy-start.5 = (f32[1024]{0:T(1024)S(1)}, f32[1024]{0:T(1024)}, u32[]{:S(2)}) copy-start(f32[1024]{0:T(1024)} %param.19) | copy-start | bytes 12292
  237.1 4.3 %copy-start.8 = (f32[1024]{0:T(1024)S(1)}, f32[1024]{0:T(1024)}, u32[]{:S(2)}) copy-start(f32[1024]{0:T(1024)} %param.17) | copy-start | bytes 12292
  237.1 39.0 %copy-start.9 = (f32[1024]{0:T(1024)S(1)}, f32[1024]{0:T(1024)}, u32[]{:S(2)}) copy-start(f32[1024]{0:T(1024)} %param.18) | copy-start | bytes 12292
Sparse Core Ops, SparseCore 0:
  126.4 22.0 all-reduce.2
where the time goes:
time: 284 us
  local copies, waits for them, and re-layouts  95.7 us (34%)
  other arithmetic  67.9 us (24%)
  waiting for transfers between devices  41.8 us (15%)
  blocking collectives  36.4 us (13%)
  starting transfers between devices  22.5 us (8%)
  between operations  19.1 us (7%)
    scatter-add x1, other arithmetic, on_device(): jnp.zeros((3, owned_nodes + ghost_slots), jnp.float32).at[:, flat_connect]  51.9 us
    gather x2, local copies, waits for them, and re-layouts, on_device(): pulled = weighted_full[:, connect].reshape(30, element_count)  40.3 us
    gather x2, local copies, waits for them, and re-layouts, on_device(): element_state = state_full[:, connect].reshape(30, element_count)  38.4 us
    psum x1, blocking collectives, on_device(): lax.psum((jnp.sum(remain * remain), jnp.sum(search * hess_search), jnp.su...  30.1 us
    psum x1, waiting for transfers between devices, on_device(): accumulated = lax.psum(accumulated, 'field')  22.3 us
    ppermute x3, waiting for transfers between devices, extended(): lax.ppermute(head, axis, [((i + 1) % count, i) for i in range(ends)])  12.5 us
    ppermute x3, starting transfers between devices, extended(): lax.ppermute(tail, axis, [(i, (i + 1) % count) for i in range(ends)])  11.1 us
    scatter-add x1, other arithmetic, on_device(): assembled = accumulated[:, :owned_nodes] + jnp.zeros((3, owned_nodes), jn...  9.52 us
  transfers between devices with their start and end apart: 9, of which 6 were waited for; matrix products, arithmetic and copies ran while one was open for 0% of the time, Pallas kernels for 0%

commit v1 on v0

--- a/solution.py
+++ b/solution.py
@@ -69,7 +69,8 @@
     accumulated = (
         jnp.zeros((3, owned_nodes + ghost_slots), jnp.float32).at[:, flat_connect].add(terms)
     )
-    accumulated = lax.psum(accumulated, "field")
+    parts = lax.all_gather(accumulated, "field", axis=0, tiled=False)
+    accumulated = parts.sum(axis=0)
     returning = accumulated[:, owned_nodes:].reshape(3, 3, sub_count, link_slots)
     rimmed = extended(returning, (("dom", 1),), 1)
     landed = lax.all_to_all(rimmed[:, 0::2], "sub", split_axis=2, concat_axis=2, tiled=True)

time: 284 us -> 249 us (0.88)
  waiting for transfers between devices: 41.8 us -> 18.9 us
  between operations: 19.1 us -> 5.65 us
    psum x1 -> x0, waiting for transfers between devices: 22.3 us -> none  [on_device(): accumulated = lax.psum(accumulated, 'field')]
  transfers between devices with their start and end apart: 9 -> 8, of which waited for: 6 -> 5; matrix products, arithmetic and copies ran while one was open for 0% -> 0% of each run, Pallas kernels for 0% -> 0%
where the time goes in v1:
time: 249 us; the launch traced here: 248 us
  local copies, waits for them, and re-layouts  95.7 us (38%)
  other arithmetic  67.1 us (27%)
  blocking collectives  38.4 us (15%)
  starting transfers between devices  22.3 us (9%)
  waiting for transfers between devices  18.9 us (8%)
  between operations  5.65 us (2%)
    scatter-add x1, other arithmetic, on_device(): jnp.zeros((3, owned_nodes + ghost_slots), jnp.float32).at[:, flat_connect]  50.9 us
    gather x2, local copies, waits for them, and re-layouts, on_device(): pulled = weighted_full[:, connect].reshape(30, element_count)  40.3 us
    gather x2, local copies, waits for them, and re-layouts, on_device(): element_state = state_full[:, connect].reshape(30, element_count)  38.5 us
    psum x1, blocking collectives, on_device(): lax.psum((jnp.sum(remain * remain), jnp.sum(search * hess_search), jnp.su...  30.1 us
    ppermute x3, waiting for transfers between devices, extended(): lax.ppermute(head, axis, [((i + 1) % count, i) for i in range(ends)])  12.5 us
    ppermute x3, starting transfers between devices, extended(): lax.ppermute(tail, axis, [(i, (i + 1) % count) for i in range(ends)])  10.9 us
    scatter-add x1, other arithmetic, on_device(): assembled = accumulated[:, :owned_nodes] + jnp.zeros((3, owned_nodes), jn...  9.52 us
    gather x2, local copies, waits for them, and re-layouts, fetch_ghosts(): values[:, targets].reshape(3, 3, sub_count, link_slots) * open_slot[None]  6.92 us
  transfers between devices with their start and end apart: 8, of which 5 were waited for; matrix products, arithmetic and copies ran while one was open for 0% of the time, Pallas kernels for 0%

profile of v1, /device:TPU:0, one launch (start us, length us, event | category | flops | bytes accessed | tf_op | source)
XLA Modules:
  0.0 248.2 jit_solution(15532677477096466108)
XLA Ops:
  0.7 0.8 reshape_squeeze.3
  1.5 0.8 fusion.4
  2.3 1.5 copy.88
  3.7 2.6 %gather_fusion = f32[1536,3]{1,0:T(8,128)S(1)} fusion(f32[3,4096]{0,1:T(8,128)S(1)} %copy.88, s32[2048]{0:T(1024)S(1)} %pad_clamp_fusion), kind=kCustom, calls=%fused_computation | custom fusion | bytes 43008 | tf_op jit(solution)/shard_map/gather | solution.py:51
  7.3 4.2 %all-to-all-start = ((f32[3,3,2,256]{3,1,0,2:T(4,128)}), f32[3,3,2,256]{3,1,0,2:T(4,128)S(1)}, u32[]{:S(2)}, u32[]{:S(2)}) async-start(f32[3,3,2,256]{3,1,0,2:T(4,128)} %broadcast_multiply_fusion.4), calls=%async_computation | async-start | bytes 49152 | tf_op jit(solution)/shard_map/all_to_all | solution.py:52
  12.3 3.1 %all-to-all-done = f32[3,3,2,256]{3,1,0,2:T(4,128)S(1)} async-done(((f32[3,3,2,256]{3,1,0,2:T(4,128)}), f32[3,3,2,256]{3,1,0,2:T(4,128)S(1)}, u32[]{:S(2)}, u32[]{:S(2)}) %all-to-all-start) | async-done | bytes 18464 | tf_op jit(solution)/shard_map/all_to_all | solution.py:52
  15.4 4.0 %collective-permute-start = (f32[3,1,2,256]{3,1,0,2:T(1,128)S(1)}, f32[3,1,2,256]{3,1,0,2:T(1,128)S(1)}, u32[]{:S(2)}, u32[]{:S(2)}) collective-permute-start(f32[3,1,2,256]{3,1,0,2:T(1,128)S(1)} %get-tuple-element.16), channel_id=1, source_target_pairs={{0,4},{4,8},{8,12},{1,5},{5,9},{9,13},{2,6},{6,10},{10,14},{3,7},{... | collective-permute-start | bytes 18440 | tf_op jit(solution)/shard_map/ppermute | solution.py:17
  19.4 1.3 collective-permute-start.1
  20.8 4.1 %collective-permute-done.1 = f32[3,1,2,256]{3,1,0,2:T(1,128)S(1)} collective-permute-done((f32[3,1,2,256]{3,1,0,2:T(1,128)S(1)}, f32[3,1,2,256]{3,1,0,2:T(1,128)S(1)}, u32[]{:S(2)}, u32[]{:S(2)}) %collective-permute-start.1) | collective-permute-done | bytes 6176 | tf_op jit(solution)/shard_map/ppermute | solution.py:19
  25.0 0.8 copy.93
  25.9 34.3 %gather_fusion.1 = f32[10240,3]{1,0:T(8,128)} fusion(f32[3,5632]{0,1:T(8,128)S(1)} %copy.93, s32[10240]{0:T(1024)S(1)} %broadcast_clamp_fusion), kind=kCustom, calls=%fused_computation.1 | custom fusion | bytes 286720 | tf_op jit(solution)/shard_map/gather | solution.py:64
  60.2 4.2 %copy.94 = f32[10,1024,3]{1,0,2:T(8,128)S(1)} copy(f32[10,1024,3]{2,1,0:T(8,128)} %bitcast.29) | data formatting | bytes 245760 | tf_op jit(solution)/shard_map/gather | solution.py:64
  64.8 3.1 %copy.95 = f32[3,10240]{0,1:T(8,128)} copy(f32[3,10240]{1,0:T(4,128)S(1)} %reshape.145) | data formatting | bytes 245760 | tf_op jit(solution)/shard_map/reshape | solution.py:68
  67.9 50.9 %scatter_custom_fusion = f32[3,5632]{0,1:T(8,128)S(1)} fusion(s32[10240]{0:T(1024)S(1)} %bitcast.38, f32[3,10240]{0,1:T(8,128)} %copy.95, f32[]{:T(128)} %constant.7.clone.1), kind=kCustom, calls=%fused_computation.6 | custom fusion | flops 30720 | bytes 190468 | tf_op jit(solution)/shard_map/scatter-add | solution.py:70
  118.8 0.8 copy.96
  119.6 2.1 all-gather.1
  121.8 3.5 %collective-permute-start.2 = (f32[3,1,2,256]{3,2,1,0:T(2,128)S(1)}, f32[3,1,2,256]{3,2,1,0:T(2,128)S(1)}, u32[]{:S(2)}, u32[]{:S(2)}) collective-permute-start(f32[3,1,2,256]{3,2,1,0:T(2,128)S(1)} %get-tuple-element.18), channel_id=1, source_target_pairs={{0,4},{4,8},{8,12},{1,5},{5,9},{9,13},{2,6},{6,10},{10,14},{3,7},{... | collective-permute-start | bytes 18440 | tf_op jit(solution)/shard_map/ppermute | solution.py:17
  125.3 1.3 collective-permute-start.3
  126.6 4.2 %collective-permute-done.3 = f32[3,1,2,256]{3,2,1,0:T(2,128)S(1)} collective-permute-done((f32[3,1,2,256]{3,2,1,0:T(2,128)S(1)}, f32[3,1,2,256]{3,2,1,0:T(2,128)S(1)}, u32[]{:S(2)}, u32[]{:S(2)}) %collective-permute-start.3) | collective-permute-done | bytes 6176 | tf_op jit(solution)/shard_map/ppermute | solution.py:19
  131.5 3.2 %all-to-all-start.1 = ((f32[3,3,2,256]{3,1,0,2:T(4,128)}), f32[3,3,2,256]{3,1,0,2:T(4,128)S(1)}, u32[]{:S(2)}, u32[]{:S(2)}) async-start(f32[3,3,2,256]{3,1,0,2:T(4,128)} %copy.107), calls=%async_computation.1 | async-start | bytes 49152 | tf_op jit(solution)/shard_map/all_to_all | solution.py:76
  135.4 3.2 %all-to-all-done.1 = f32[3,3,2,256]{3,1,0,2:T(4,128)S(1)} async-done(((f32[3,3,2,256]{3,1,0,2:T(4,128)}), f32[3,3,2,256]{3,1,0,2:T(4,128)S(1)}, u32[]{:S(2)}, u32[]{:S(2)}) %all-to-all-start.1) | async-done | bytes 18464 | tf_op jit(solution)/shard_map/all_to_all | solution.py:76
  139.0 9.5 %scatter_fusion = f32[3,4096]{0,1:T(8,128)S(1)} fusion(f32[3,4096]{0,1:T(8,128)S(1)} %copy.99, s32[1536]{0:T(1024)S(1)} %fusion.5, f32[1536,3]{1,0:T(8,128)S(1)} %copy.100), kind=kCustom, calls=%fused_computation.5 | custom fusion | flops 4608 | bytes 61440 | tf_op jit(solution)/shard_map/scatter-add | solution.py:80
  148.5 2.0 broadcast_multiply_fusion
  150.5 4.3 %gather_fusion.2 = f32[1536,3]{1,0:T(8,128)S(1)} fusion(f32[3,4096]{0,1:T(8,128)} %broadcast_multiply_fusion, s32[2048]{0:T(1024)S(1)} %pad_clamp_fusion), kind=kCustom, calls=%fused_computation.2 | custom fusion | bytes 43008 | tf_op jit(solution)/shard_map/gather | solution.py:51
  155.1 6.3 %all_to_all.15 = f32[3,3,2,256]{3,1,0,2:T(4,128)S(1)} all-to-all(f32[3,3,2,256]{3,1,0,2:T(4,128)S(1)} %broadcast_multiply_fusion.2), channel_id=1, replica_groups=mesh['groups'=2,'dom'=4,'sub'=2,'field'=2] {'sub'}, dimensions={2} | all-to-all | bytes 36864 | tf_op jit(solution)/shard_map/all_to_all | solution.py:52
  161.4 3.5 %collective-permute-start.4 = (f32[3,1,2,256]{3,1,0,2:T(1,128)S(1)}, f32[3,1,2,256]{3,1,0,2:T(1,128)S(1)}, u32[]{:S(2)}, u32[]{:S(2)}) collective-permute-start(f32[3,1,2,256]{3,1,0,2:T(1,128)S(1)} %get-tuple-element.14), channel_id=1, source_target_pairs={{0,4},{4,8},{8,12},{1,5},{5,9},{9,13},{2,6},{6,10},{10,14},{3,7},{... | collective-permute-start | bytes 18440 | tf_op jit(solution)/shard_map/ppermute | solution.py:17
  164.9 1.3 collective-permute-start.5
  166.3 4.2 %collective-permute-done.5 = f32[3,1,2,256]{3,1,0,2:T(1,128)S(1)} collective-permute-done((f32[3,1,2,256]{3,1,0,2:T(1,128)S(1)}, f32[3,1,2,256]{3,1,0,2:T(1,128)S(1)}, u32[]{:S(2)}, u32[]{:S(2)}) %collective-permute-start.5) | collective-permute-done | bytes 6176 | tf_op jit(solution)/shard_map/ppermute | solution.py:19
  170.8 1.7 pad_maximum_fusion
  172.5 36.1 %gather_fusion.3 = f32[10240,3]{1,0:T(8,128)} fusion(f32[3,5632]{0,1:T(8,128)} %pad_maximum_fusion, s32[10240]{0:T(1024)S(1)} %broadcast_clamp_fusion), kind=kCustom, calls=%fused_computation.3 | custom fusion | bytes 286720 | tf_op jit(solution)/shard_map/gather | solution.py:83
  208.6 4.2 %copy.106 = f32[10,1024,3]{1,0,2:T(8,128)S(1)} copy(f32[10,1024,3]{2,1,0:T(8,128)} %bitcast.28) | data formatting | bytes 245760 | tf_op jit(solution)/shard_map/gather | solution.py:83
  213.6 30.1 %all-reduce = (f32[]{:T(128)}, f32[]{:T(128)}, f32[]{:T(128)}, f32[]{:T(128)}) all-reduce(f32[]{:T(128)} %get-tuple-element.5, f32[]{:T(128)} %get-tuple-element.6, f32[]{:T(128)} %get-tuple-element.4, f32[]{:T(128)} %get-tuple-element.3), channel_id=1, replica_groups=mesh['groups'=2,'dom'=4,'sub'=2,'field'=2] {'dom','sub','field'}, use_global_device_ids=true, to_apply=%region_1.0 | all-reduce | flops 4 | bytes 32 | tf_op jit(solution)/shard_map/psum | solution.py:85
  (70 shorter events, 5.4 us)
Async XLA Ops:
  0.6 63.8 %copy-start = (f32[30,30]{1,0:T(8,128)S(1)}, f32[30,30]{1,0:T(8,128)}, u32[]{:S(2)}) copy-start(f32[30,30]{1,0:T(8,128)} %param.23) | copy-start | bytes 10804
  0.6 24.3 %copy-start.2 = (f32[3,4096]{1,0:T(4,128)S(1)}, f32[3,4096]{1,0:T(4,128)}, u32[]{:S(2)}) copy-start(f32[3,4096]{1,0:T(4,128)} %param.12) | copy-start | bytes 147460
  0.7 10.9 %copy-start.3 = (s32[10,1024]{1,0:T(8,128)S(1)}, s32[10,1024]{1,0:T(8,128)}, u32[]{:S(2)}) copy-start(s32[10,1024]{1,0:T(8,128)} %param.14) | copy-start | bytes 122884
  0.7 20.0 %copy-start.7 = (f32[1024]{0:T(1024)S(1)}, f32[1024]{0:T(1024)}, u32[]{:S(2)}) copy-start(f32[1024]{0:T(1024)} %param.20) | copy-start | bytes 12292
  0.7 20.0 %copy-start.6 = (f32[1024]{0:T(1024)S(1)}, f32[1024]{0:T(1024)}, u32[]{:S(2)}) copy-start(f32[1024]{0:T(1024)} %param.16) | copy-start | bytes 12292
  7.3 8.1 %all-to-all-start = ((f32[3,3,2,256]{3,1,0,2:T(4,128)}), f32[3,3,2,256]{3,1,0,2:T(4,128)S(1)}, u32[]{:S(2)}, u32[]{:S(2)}) async-start(f32[3,3,2,256]{3,1,0,2:T(4,128)} %broadcast_multiply_fusion.4), calls=%async_computation | async-start | bytes 49152 | tf_op jit(solution)/shard_map/all_to_all | solution.py:52
  15.4 5.3 %collective-permute-start = (f32[3,1,2,256]{3,1,0,2:T(1,128)S(1)}, f32[3,1,2,256]{3,1,0,2:T(1,128)S(1)}, u32[]{:S(2)}, u32[]{:S(2)}) collective-permute-start(f32[3,1,2,256]{3,1,0,2:T(1,128)S(1)} %get-tuple-element.16), channel_id=1, source_target_pairs={{0,4},{4,8},{8,12},{1,5},{5,9},{9,13},{2,6},{6,10},{10,14},{3,7},{... | collective-permute-start | bytes 18440 | tf_op jit(solution)/shard_map/ppermute | solution.py:17
  19.4 5.5 %collective-permute-start.1 = (f32[3,1,2,256]{3,1,0,2:T(1,128)S(1)}, f32[3,1,2,256]{3,1,0,2:T(1,128)S(1)}, u32[]{:S(2)}, u32[]{:S(2)}) collective-permute-start(f32[3,1,2,256]{3,1,0,2:T(1,128)S(1)} %get-tuple-element.17), channel_id=1, source_target_pairs={{4,0},{8,4},{12,8},{5,1},{9,5},{13,9},{6,2},{10,6},{14,10},{7,3},{... | collective-permute-start | bytes 18440 | tf_op jit(solution)/shard_map/ppermute | solution.py:19
  119.6 28.8 %copy-start.4 = (f32[4096]{0:T(1024)S(1)}, f32[4096]{0:T(1024)}, u32[]{:S(2)}) copy-start(f32[4096]{0:T(1024)} %param.13) | copy-start | bytes 49156
  121.8 4.8 %collective-permute-start.2 = (f32[3,1,2,256]{3,2,1,0:T(2,128)S(1)}, f32[3,1,2,256]{3,2,1,0:T(2,128)S(1)}, u32[]{:S(2)}, u32[]{:S(2)}) collective-permute-start(f32[3,1,2,256]{3,2,1,0:T(2,128)S(1)} %get-tuple-element.18), channel_id=1, source_target_pairs={{0,4},{4,8},{8,12},{1,5},{5,9},{9,13},{2,6},{6,10},{10,14},{3,7},{... | collective-permute-start | bytes 18440 | tf_op jit(solution)/shard_map/ppermute | solution.py:17
  125.3 5.5 %collective-permute-start.3 = (f32[3,1,2,256]{3,2,1,0:T(2,128)S(1)}, f32[3,1,2,256]{3,2,1,0:T(2,128)S(1)}, u32[]{:S(2)}, u32[]{:S(2)}) collective-permute-start(f32[3,1,2,256]{3,2,1,0:T(2,128)S(1)} %get-tuple-element.19), channel_id=1, source_target_pairs={{4,0},{8,4},{12,8},{5,1},{9,5},{13,9},{6,2},{10,6},{14,10},{7,3},{... | collective-permute-start | bytes 18440 | tf_op jit(solution)/shard_map/ppermute | solution.py:19
  131.5 7.1 %all-to-all-start.1 = ((f32[3,3,2,256]{3,1,0,2:T(4,128)}), f32[3,3,2,256]{3,1,0,2:T(4,128)S(1)}, u32[]{:S(2)}, u32[]{:S(2)}) async-start(f32[3,3,2,256]{3,1,0,2:T(4,128)} %copy.107), calls=%async_computation.1 | async-start | bytes 49152 | tf_op jit(solution)/shard_map/all_to_all | solution.py:76
  150.5 20.3 %copy-start.1 = (f32[3,4096]{0,1:T(8,128)S(1)}, f32[3,4096]{0,1:T(8,128)}, u32[]{:S(2)}) copy-start(f32[3,4096]{0,1:T(8,128)} %broadcast_multiply_fusion) | copy-start | bytes 147460
  161.4 4.8 %collective-permute-start.4 = (f32[3,1,2,256]{3,1,0,2:T(1,128)S(1)}, f32[3,1,2,256]{3,1,0,2:T(1,128)S(1)}, u32[]{:S(2)}, u32[]{:S(2)}) collective-permute-start(f32[3,1,2,256]{3,1,0,2:T(1,128)S(1)} %get-tuple-element.14), channel_id=1, source_target_pairs={{0,4},{4,8},{8,12},{1,5},{5,9},{9,13},{2,6},{6,10},{10,14},{3,7},{... | collective-permute-start | bytes 18440 | tf_op jit(solution)/shard_map/ppermute | solution.py:17
  164.9 5.5 %collective-permute-start.5 = (f32[3,1,2,256]{3,1,0,2:T(1,128)S(1)}, f32[3,1,2,256]{3,1,0,2:T(1,128)S(1)}, u32[]{:S(2)}, u32[]{:S(2)}) collective-permute-start(f32[3,1,2,256]{3,1,0,2:T(1,128)S(1)} %get-tuple-element.15), channel_id=1, source_target_pairs={{4,0},{8,4},{12,8},{5,1},{9,5},{13,9},{6,2},{10,6},{14,10},{7,3},{... | collective-permute-start | bytes 18440 | tf_op jit(solution)/shard_map/ppermute | solution.py:19
  208.6 4.3 %copy-start.5 = (f32[1024]{0:T(1024)S(1)}, f32[1024]{0:T(1024)}, u32[]{:S(2)}) copy-start(f32[1024]{0:T(1024)} %param.19) | copy-start | bytes 12292
  208.6 4.3 %copy-start.8 = (f32[1024]{0:T(1024)S(1)}, f32[1024]{0:T(1024)}, u32[]{:S(2)}) copy-start(f32[1024]{0:T(1024)} %param.17) | copy-start | bytes 12292
  208.6 39.0 %copy-start.9 = (f32[1024]{0:T(1024)S(1)}, f32[1024]{0:T(1024)}, u32[]{:S(2)}) copy-start(f32[1024]{0:T(1024)} %param.18) | copy-start | bytes 12292
